TPU v7x, 32 devices: a whole 2x2x4 slice. The times are simulated.
32 devices in a mesh: row: 8 (over y, x, core), col: 4 (over z).
Axes of the slice: x: 2, y: 2, z: 4, core: 2. Of those that a mesh axis runs over, the one named last changes fastest.
Arguments:
- tokens: bfloat16 [32, 8192], P(None, 'row'), may hold values from -6 to 6
- gain: float32 [8192], P('row'), may hold values from 0.24 to 4.5
- gate_weight: bfloat16 [8192, 28672], P('row', 'col'), may hold values from -0.0625 to 0.0625
- up_weight: bfloat16 [8192, 28672], P('row', 'col'), may hold values from -0.0625 to 0.0625
- down_weight: bfloat16 [28672, 8192], P('col', 'row'), may hold values from -0.03125 to 0.03125
- probes: float32 [4, 32, 8192], P(None, None, 'row'), may hold values from -6 to 6
Outputs:
- basis: float32 [4, 32, 8192], P(None, None, 'row')
- stretch: float32 [4], replicated
All inputs are finite; a program needn't handle non-finite values.
Results may differ from a plain program's by a relative error of at most 0.0085.
Values may be sent and summed in bfloat16 or wider, within the bound.
No kernel may reach another device: no remote copies, remote signals or barrier semaphores. Data moves between devices by JAX's collectives and lax.ppermute only.
A program may use at most 128 MiB of HBM per device.

v0:
```python
import jax
import jax.numpy as jnp
from jax import lax
from jax.sharding import PartitionSpec as P

ITERS = 3
epsilon = 1e-06


def local(tokens, gain, gate_weight, up_weight, down_weight, probes):
    scaled = (tokens.astype(jnp.float32) * gain).astype(jnp.bfloat16)
    gate_part = jnp.dot(scaled, gate_weight, preferred_element_type=jnp.float32)
    up_part = jnp.dot(scaled, up_weight, preferred_element_type=jnp.float32)
    gate, up = lax.psum((gate_part, up_part), "row")
    sigmoid_gate = 1.0 / (1.0 + jnp.exp(-gate))
    activated = gate * sigmoid_gate
    slope = sigmoid_gate * (1.0 + gate * (1.0 - sigmoid_gate)) * up
    probe_count, token_count, local_width = probes.shape
    row_count = probe_count * token_count
    slope_all = jnp.tile(slope, (probe_count, 1))
    activated_all = jnp.tile(activated, (probe_count, 1))
    entries = token_count * local_width * lax.axis_size("row")
    transposed = (((1,), (1,)), ((), ()))
    current = probes
    level = jnp.zeros((probe_count,), jnp.float32)
    for sweep in range(ITERS):
        pushed = (current * gain).astype(jnp.bfloat16).reshape(row_count, local_width)
        gate_tan = jnp.dot(pushed, gate_weight, preferred_element_type=jnp.float32)
        up_tan = jnp.dot(pushed, up_weight, preferred_element_type=jnp.float32)
        joined = slope_all * gate_tan + activated_all * up_tan
        hidden = lax.psum_scatter(joined, "row", scatter_dimension=0, tiled=True).astype(
            jnp.bfloat16
        )
        tangent_part = jnp.dot(
            lax.all_gather(hidden, "row", axis=0, tiled=True),
            down_weight,
            preferred_element_type=jnp.float32,
        )
        tangent = lax.psum(tangent_part, "col").astype(jnp.bfloat16)
        back_part = lax.dot_general(
            tangent, down_weight, transposed, preferred_element_type=jnp.float32
        )
        back = lax.psum(back_part, "row").astype(jnp.bfloat16)
        gate_pull = (slope_all * back).astype(jnp.bfloat16)
        up_pull = (activated_all * back).astype(jnp.bfloat16)
        result = lax.dot_general(
            gate_pull, gate_weight, transposed, preferred_element_type=jnp.float32
        )
        pulled_part = result + lax.dot_general(
            up_pull, up_weight, transposed, preferred_element_type=jnp.float32
        )
        pulled = lax.psum(pulled_part, "col")
        grown = pulled.reshape(probe_count, token_count, local_width) * gain
        squares = jnp.sum(grown * grown, axis=(1, 2))
        level = lax.psum(squares, "row") / entries
        current = grown * lax.rsqrt(level + epsilon)[:, None, None]
    return (current, jnp.sqrt(level))


def solution(mesh):
    placed = (
        P(None, "row"),
        P("row"),
        P("row", "col"),
        P("row", "col"),
        P("col", "row"),
        P(None, None, "row"),
    )
    return jax.shard_map(
        local, mesh=mesh, in_specs=placed, out_specs=(P(None, None, "row"), P()), check_vma=False
    )
```

profile of v0, /device:TPU:0, one launch (start us, length us, event | category | flops | bytes accessed | tf_op | source)
XLA Modules:
  0.0 980.3 jit_solution(12763348402583226516)
XLA Ops:
  7.2 8.9 fusion.16
  16.2 0.8 copy-done
  17.0 3.6 fusion.17
  20.7 63.1 %all-reduce.18.cloned.1.call-done = (f32[32,7168]{1,0:T(8,128)}, f32[32,7168]{1,0:T(8,128)}) async-done(((f32[32,7168]{1,0:T(8,128)}, f32[32,7168]{1,0:T(8,128)}), (f32[32,7168]{1,0:T(8,128)}, f32[32,7168]{1,0:T(8,128)})) %all-reduce.18.cloned.1.call-update) | async-done | bytes 1835024 | tf_op jit(solution)/shard_map/psum | solution.py:14
  83.7 1.8 fusion.9
  85.6 7.3 bitcast_multiply_fusion.5
  92.8 9.3 fusion
  102.2 47.9 %reduce-scatter.4.cloned.1.call-done = f32[16,7168]{1,0:T(8,128)} async-done(((f32[128,7168]{1,0:T(8,128)}), f32[16,7168]{1,0:T(8,128)}) %reduce-scatter.4.cloned.1.call-update) | async-done | bytes 458768 | tf_op jit(solution)/shard_map/reduce_scatter | solution.py:31
  150.1 1.7 convert_element_type.77
  151.9 27.4 %all-gather.4.cloned.1.call-done = bf16[128,7168]{1,0:T(8,128)(2,1)} async-done(((bf16[16,7168]{1,0:T(8,128)(2,1)}), bf16[128,7168]{1,0:T(8,128)(2,1)}) %all-gather.4.cloned.1.call-update) | async-done | bytes 1835024 | tf_op jit(solution)/shard_map/all_gather | solution.py:35
  179.3 7.8 fusion.18
  187.1 30.6 %all-reduce.19 = bf16[128,1024]{1,0:T(8,128)(2,1)S(1)} all-reduce(f32[128,1024]{1,0:T(8,128)S(1)} %fusion.18), channel_id=1, replica_groups=mesh['row'=8,'col'=4] {'col'}, use_global_device_ids=true, to_apply=%region_3.0 | all-reduce | flops 131072 | bytes 786432 | tf_op jit(solution)/shard_map/psum | solution.py:39
  217.7 11.8 %fusion.26 = f32[128,7168]{1,0:T(8,128)} fusion(bf16[128,1024]{1,0:T(8,128)(2,1)S(1)} %all-reduce.19, bf16[7168,1024]{1,0:T(8,128)(2,1)} %param.10), kind=kOutput, calls=%fused_computation.55 | convolution fusion | flops 1879048192 | bytes 18612224 | tf_op jit(solution)/shard_map/dot_general | solution.py:40
  229.5 77.7 %all-reduce.20 = bf16[128,7168]{1,0:T(8,128)(2,1)} all-reduce(f32[128,7168]{1,0:T(8,128)} %fusion.26), channel_id=1, replica_groups=mesh['row'=8,'col'=4] {'row'}, use_global_device_ids=true, to_apply=%region_4.0 | all-reduce | flops 917504 | bytes 5505024 | tf_op jit(solution)/shard_map/psum | solution.py:43
  307.2 2.1 fusion.6
  309.4 10.1 %fusion.19 = f32[128,1024]{1,0:T(8,128)S(1)} fusion(bf16[128,7168]{1,0:T(8,128)(2,1)S(1)} %get-tuple-element.9, bf16[1024,7168]{1,0:T(8,128)(2,1)} %param.8), kind=kOutput, calls=%fused_computation.48 | convolution fusion | flops 1879048192 | bytes 17039360 | tf_op jit(solution)/shard_map/dot_general | solution.py:46
  319.5 10.9 %convolution_add_fusion.2 = f32[128,1024]{1,0:T(8,128)} fusion(f32[128,1024]{1,0:T(8,128)S(1)} %fusion.19, bf16[128,7168]{1,0:T(8,128)(2,1)S(1)} %get-tuple-element.8, bf16[1024,7168]{1,0:T(8,128)(2,1)} %param.9), kind=kOutput, calls=%fused_computation.23 | convolution fusion | flops 1879179264 | bytes 17563648 | tf_op jit(solution)/shard_map/dot_general | solution.py:49
  330.4 0.0 reduce-scatter.6.cloned.1.call-start
  330.5 36.4 %all-reduce.12.cloned.1.call-done = f32[128,1024]{1,0:T(8,128)} async-done(((f32[128,1024]{1,0:T(8,128)}), f32[128,1024]{1,0:T(8,128)}) %all-reduce.12.cloned.1.call-update) | async-done | bytes 524304 | tf_op jit(solution)/shard_map/psum | solution.py:52
  366.9 1.2 multiply_reduce_fusion.2
  368.1 0.1 reduce_sum.37
  368.2 0.1 reduce_sum.38
  368.3 13.1 %psum.103 = f32[4]{0:T(128)S(1)} all-reduce(f32[4]{0:T(128)S(1)} %reduce_sum.38), channel_id=1, replica_groups=mesh['row'=8,'col'=4] {'row'}, use_global_device_ids=true, to_apply=%region_8.0 | all-reduce | flops 4 | bytes 32 | tf_op jit(solution)/shard_map/psum | solution.py:55
  381.4 0.1 mul.166
  381.5 0.1 mul.167
  381.6 7.5 bitcast_multiply_fusion.3
  389.1 9.3 fusion.1
  398.5 0.0 all-gather.6.cloned.1.call-start
  398.5 46.7 %reduce-scatter.6.cloned.1.call-done = f32[16,7168]{1,0:T(8,128)} async-done(((f32[128,7168]{1,0:T(8,128)}), f32[16,7168]{1,0:T(8,128)}) %reduce-scatter.6.cloned.1.call-update) | async-done | bytes 458768 | tf_op jit(solution)/shard_map/reduce_scatter | solution.py:31
  445.2 1.7 convert_element_type.84
  447.0 27.2 %all-gather.6.cloned.1.call-done = bf16[128,7168]{1,0:T(8,128)(2,1)} async-done(((bf16[16,7168]{1,0:T(8,128)(2,1)}), bf16[128,7168]{1,0:T(8,128)(2,1)}) %all-gather.6.cloned.1.call-update) | async-done | bytes 1835024 | tf_op jit(solution)/shard_map/all_gather | solution.py:35
  474.3 7.8 fusion.20
  482.1 30.4 %all-reduce.21 = bf16[128,1024]{1,0:T(8,128)(2,1)S(1)} all-reduce(f32[128,1024]{1,0:T(8,128)S(1)} %fusion.20), channel_id=1, replica_groups=mesh['row'=8,'col'=4] {'col'}, use_global_device_ids=true, to_apply=%region_10.0 | all-reduce | flops 131072 | bytes 786432 | tf_op jit(solution)/shard_map/psum | solution.py:39
  512.4 11.8 %fusion.25 = f32[128,7168]{1,0:T(8,128)} fusion(bf16[128,1024]{1,0:T(8,128)(2,1)S(1)} %all-reduce.21, bf16[7168,1024]{1,0:T(8,128)(2,1)} %param.10), kind=kOutput, calls=%fused_computation.54 | convolution fusion | flops 1879048192 | bytes 18612224 | tf_op jit(solution)/shard_map/dot_general | solution.py:40
  524.3 77.9 %all-reduce.22 = bf16[128,7168]{1,0:T(8,128)(2,1)} all-reduce(f32[128,7168]{1,0:T(8,128)} %fusion.25), channel_id=1, replica_groups=mesh['row'=8,'col'=4] {'row'}, use_global_device_ids=true, to_apply=%region_11.0 | all-reduce | flops 917504 | bytes 5505024 | tf_op jit(solution)/shard_map/psum | solution.py:43
  602.2 2.1 fusion.7
  604.3 10.1 %fusion.21 = f32[128,1024]{1,0:T(8,128)S(1)} fusion(bf16[128,7168]{1,0:T(8,128)(2,1)S(1)} %get-tuple-element.7, bf16[1024,7168]{1,0:T(8,128)(2,1)} %param.8), kind=kOutput, calls=%fused_computation.50 | convolution fusion | flops 1879048192 | bytes 17039360 | tf_op jit(solution)/shard_map/dot_general | solution.py:46
  614.4 10.9 %convolution_add_fusion.1 = f32[128,1024]{1,0:T(8,128)} fusion(f32[128,1024]{1,0:T(8,128)S(1)} %fusion.21, bf16[128,7168]{1,0:T(8,128)(2,1)S(1)} %get-tuple-element.6, bf16[1024,7168]{1,0:T(8,128)(2,1)} %param.9), kind=kOutput, calls=%fused_computation.22 | convolution fusion | flops 1879179264 | bytes 17563648 | tf_op jit(solution)/shard_map/dot_general | solution.py:49
  625.4 36.3 %all-reduce.14.cloned.1.call-done = f32[128,1024]{1,0:T(8,128)} async-done(((f32[128,1024]{1,0:T(8,128)}), f32[128,1024]{1,0:T(8,128)}) %all-reduce.14.cloned.1.call-update) | async-done | bytes 524304 | tf_op jit(solution)/shard_map/psum | solution.py:52
  661.7 1.2 multiply_reduce_fusion.1
  662.9 0.1 reduce_sum.40
  662.9 0.1 reduce_sum.44
  663.1 12.9 %psum.107 = f32[4]{0:T(128)S(1)} all-reduce(f32[4]{0:T(128)S(1)} %reduce_sum.44), channel_id=1, replica_groups=mesh['row'=8,'col'=4] {'row'}, use_global_device_ids=true, to_apply=%region_15.0 | all-reduce | flops 4 | bytes 32 | tf_op jit(solution)/shard_map/psum | solution.py:55
  676.0 0.1 mul.177
  676.1 0.1 mul.178
  676.2 7.5 bitcast_multiply_fusion.1
  683.7 9.3 fusion.2
  693.1 46.7 %reduce-scatter.8.cloned.1.call-done = f32[16,7168]{1,0:T(8,128)} async-done(((f32[128,7168]{1,0:T(8,128)}), f32[16,7168]{1,0:T(8,128)}) %reduce-scatter.8.cloned.1.call-update) | async-done | bytes 458768 | tf_op jit(solution)/shard_map/reduce_scatter | solution.py:31
  739.8 1.7 convert_element_type.91
  741.6 27.4 %all-gather.8.cloned.1.call-done = bf16[128,7168]{1,0:T(8,128)(2,1)} async-done(((bf16[16,7168]{1,0:T(8,128)(2,1)}), bf16[128,7168]{1,0:T(8,128)(2,1)}) %all-gather.8.cloned.1.call-update) | async-done | bytes 1835024 | tf_op jit(solution)/shard_map/all_gather | solution.py:35
  769.0 7.8 fusion.22
  776.8 30.4 %all-reduce.23 = bf16[128,1024]{1,0:T(8,128)(2,1)S(1)} all-reduce(f32[128,1024]{1,0:T(8,128)S(1)} %fusion.22), channel_id=1, replica_groups=mesh['row'=8,'col'=4] {'col'}, use_global_device_ids=true, to_apply=%region_17.0 | all-reduce | flops 131072 | bytes 786432 | tf_op jit(solution)/shard_map/psum | solution.py:39
  807.1 11.8 %fusion.24 = f32[128,7168]{1,0:T(8,128)} fusion(bf16[128,1024]{1,0:T(8,128)(2,1)S(1)} %all-reduce.23, bf16[7168,1024]{1,0:T(8,128)(2,1)} %param.10), kind=kOutput, calls=%fused_computation.53 | convolution fusion | flops 1879048192 | bytes 18612224 | tf_op jit(solution)/shard_map/dot_general | solution.py:40
  819.0 78.0 %all-reduce.24 = bf16[128,7168]{1,0:T(8,128)(2,1)} all-reduce(f32[128,7168]{1,0:T(8,128)} %fusion.24), channel_id=1, replica_groups=mesh['row'=8,'col'=4] {'row'}, use_global_device_ids=true, to_apply=%region_18.0 | all-reduce | flops 917504 | bytes 5505024 | tf_op jit(solution)/shard_map/psum | solution.py:43
  897.0 2.1 fusion.8
  899.1 10.1 %fusion.23 = f32[128,1024]{1,0:T(8,128)S(1)} fusion(bf16[128,7168]{1,0:T(8,128)(2,1)S(1)} %get-tuple-element.5, bf16[1024,7168]{1,0:T(8,128)(2,1)} %param.8), kind=kOutput, calls=%fused_computation.52 | convolution fusion | flops 1879048192 | bytes 17039360 | tf_op jit(solution)/shard_map/dot_general | solution.py:46
  909.2 10.9 %convolution_add_fusion = f32[128,1024]{1,0:T(8,128)} fusion(f32[128,1024]{1,0:T(8,128)S(1)} %fusion.23, bf16[128,7168]{1,0:T(8,128)(2,1)S(1)} %get-tuple-element.4, bf16[1024,7168]{1,0:T(8,128)(2,1)} %param.9), kind=kOutput, calls=%fused_computation.21 | convolution fusion | flops 1879179264 | bytes 17563648 | tf_op jit(solution)/shard_map/dot_general | solution.py:49
  920.2 36.3 %all-reduce.16.cloned.1.call-done = f32[128,1024]{1,0:T(8,128)} async-done(((f32[128,1024]{1,0:T(8,128)}), f32[128,1024]{1,0:T(8,128)}) %all-reduce.16.cloned.1.call-update) | async-done | bytes 524304 | tf_op jit(solution)/shard_map/psum | solution.py:52
  956.5 1.2 multiply_reduce_fusion
  957.6 0.1 reduce_sum.55
  957.7 0.1 reduce_sum.56
  957.8 12.7 %psum.111 = f32[4]{0:T(128)S(1)} all-reduce(f32[4]{0:T(128)S(1)} %reduce_sum.56), channel_id=1, replica_groups=mesh['row'=8,'col'=4] {'row'}, use_global_device_ids=true, to_apply=%region_22.23 | all-reduce | flops 4 | bytes 32 | tf_op jit(solution)/shard_map/psum | solution.py:55
  970.6 0.5 multiply_sqrt_fusion
  971.1 2.0 multiply_multiply_fusion.1
  (32 shorter events, 0.6 us)
Async XLA Ops:
  7.2 9.0 copy-start.3
  7.2 9.0 copy-start.5
  7.2 76.6 %all-reduce.18.cloned.1.call-start = ((), (), s32[]{:S(2)}) async-start(), calls=%async_computation.12 | async-start | bytes 3670016 | tf_op jit(solution)/shard_map/psum | solution.py:14
  7.2 9.7 copy-start
  17.0 3.7 copy-start.4
  20.6 129.5 %reduce-scatter.4.cloned.1.call-start = ((), (), s32[]{:S(2)}) async-start(), calls=%async_computation.3 | async-start | bytes 4128768 | tf_op jit(solution)/shard_map/reduce_scatter | solution.py:31
  102.2 77.1 %all-gather.4.cloned.1.call-start = ((), (), s32[]{:S(2)}) async-start(), calls=%async_computation.4 | async-start | bytes 2064384 | tf_op jit(solution)/shard_map/all_gather | solution.py:35
  151.8 215.0 %all-reduce.12.cloned.1.call-start = ((), (), s32[]{:S(2)}) async-start(), calls=%async_computation.5 | async-start | bytes 1048576 | tf_op jit(solution)/shard_map/psum | solution.py:52
  330.4 114.8 %reduce-scatter.6.cloned.1.call-start = ((), (), s32[]{:S(2)}) async-start(), calls=%async_computation.6 | async-start | bytes 4128768 | tf_op jit(solution)/shard_map/reduce_scatter | solution.py:31
  381.6 7.6 copy-start.1
  398.5 75.8 %all-gather.6.cloned.1.call-start = ((), (), s32[]{:S(2)}) async-start(), calls=%async_computation.7 | async-start | bytes 2064384 | tf_op jit(solution)/shard_map/all_gather | solution.py:35
  447.0 214.7 %all-reduce.14.cloned.1.call-start = ((), (), s32[]{:S(2)}) async-start(), calls=%async_computation.8 | async-start | bytes 1048576 | tf_op jit(solution)/shard_map/psum | solution.py:52
  625.4 114.4 %reduce-scatter.8.cloned.1.call-start = ((), (), s32[]{:S(2)}) async-start(), calls=%async_computation.9 | async-start | bytes 4128768 | tf_op jit(solution)/shard_map/reduce_scatter | solution.py:31
  676.2 7.6 copy-start.2
  693.1 75.9 %all-gather.8.cloned.1.call-start = ((), (), s32[]{:S(2)}) async-start(), calls=%async_computation.10 | async-start | bytes 2064384 | tf_op jit(solution)/shard_map/all_gather | solution.py:35
  741.6 214.9 %all-reduce.16.cloned.1.call-start = ((), (), s32[]{:S(2)}) async-start(), calls=%async_computation.11 | async-start | bytes 1048576 | tf_op jit(solution)/shard_map/psum | solution.py:52
Sparse Core Ops, SparseCore 0:
  20.7 63.0 all-reduce.17
  102.3 47.7 reduce-scatter.3
  152.6 26.6 all-gather.3
  330.5 36.3 all-reduce.11
  398.6 46.5 reduce-scatter.5
  447.5 26.6 all-gather.5
  625.5 36.1 all-reduce.13
  693.2 46.5 reduce-scatter.7
  742.3 26.6 all-gather.7
  920.3 36.1 all-reduce.15
where the time goes:
time: 989 us; the launch traced here: 980 us
  waiting for transfers between devices  395 us (40%)
  blocking collectives  364 us (37%)
  matrix products  185 us (19%)
  other arithmetic  19.9 us (2%)
  between operations  14.8 us (1%)
    psum x3, blocking collectives, local(): back = lax.psum(back_part, 'row').astype(jnp.bfloat16)  234 us
    reduce_scatter x3, waiting for transfers between devices, local(): lax.psum_scatter(joined, 'row', scatter_dimension=0, tiled=True)  141 us
    psum x3, waiting for transfers between devices, local(): pulled = lax.psum(pulled_part, 'col')  109 us
    psum x3, blocking collectives, local(): tangent = lax.psum(tangent_part, 'col').astype(jnp.bfloat16)  91.3 us
    all_gather x3, waiting for transfers between devices, local(): lax.all_gather(hidden, 'row', axis=0, tiled=True)  82 us
    psum x1, waiting for transfers between devices, local(): gate, up = lax.psum((gate_part, up_part), 'row')  63.1 us
    psum x3, blocking collectives, local(): level = lax.psum(squares, 'row') / entries  38.8 us
    dot_general x3, matrix products, local(): lax.dot_general(tangent, down_weight, transposed, preferred_element_type=...  35.5 us
  transfers between devices with their start and end apart: 10, of which 10 were waited for; matrix products, arithmetic and copies ran while one was open for 0% of the time, Pallas kernels for 0%

commit v1 on v0

--- a/solution.py
+++ b/solution.py
@@ -1,3 +1,4 @@
+import functools
 import jax
 import jax.numpy as jnp
 from jax import lax
@@ -5,6 +6,14 @@
 
 ITERS = 3
 epsilon = 1e-06
+
+
+def produce_local_data_by_axis(page, shard_axis):
+    x_now = lax.all_gather(page, shard_axis)
+    return jnp.sum(x_now, axis=0)
+
+
+load_flows = functools.partial(produce_local_data_by_axis, shard_axis="col")
 
 
 def local(tokens, gain, gate_weight, up_weight, down_weight, probes):
@@ -36,7 +45,7 @@
             down_weight,
             preferred_element_type=jnp.float32,
         )
-        tangent = lax.psum(tangent_part, "col").astype(jnp.bfloat16)
+        tangent = load_flows(tangent_part).astype(jnp.bfloat16)
         back_part = lax.dot_general(
             tangent, down_weight, transposed, preferred_element_type=jnp.float32
         )

time: 989 us -> 1050 us (1.062)
  waiting for transfers between devices: 395 us -> 533 us
  blocking collectives: 364 us -> 274 us
    all_gather x0 -> x3, waiting for transfers between devices: none -> 137 us  [produce_local_data_by_axis(): x_now = lax.all_gather(page, shard_axis)]
    psum x3 -> x0, blocking collectives: 91.3 us -> none  [local(): tangent = lax.psum(tangent_part, 'col').astype(jnp.bfloat16)]
  transfers between devices with their start and end apart: 10 -> 13, of which waited for: 10 -> 13; matrix products, arithmetic and copies ran while one was open for 0% -> 0% of each run, Pallas kernels for 0% -> 0%
where the time goes in v1:
time: 1050 us; the launch traced here: 1040 us
  waiting for transfers between devices  533 us (51%)
  blocking collectives  274 us (26%)
  matrix products  187 us (18%)
  other arithmetic  25.3 us (2%)
  between operations  14.5 us (1%)
    psum x3, blocking collectives, local(): back = lax.psum(back_part, 'row').astype(jnp.bfloat16)  235 us
    reduce_scatter x3, waiting for transfers between devices, local(): lax.psum_scatter(joined, 'row', scatter_dimension=0, tiled=True)  141 us
    all_gather x3, waiting for transfers between devices, produce_local_data_by_axis(): x_now = lax.all_gather(page, shard_axis)  137 us
    psum x3, waiting for transfers between devices, local(): pulled = lax.psum(pulled_part, 'col')  110 us
    all_gather x3, waiting for transfers between devices, local(): lax.all_gather(hidden, 'row', axis=0, tiled=True)  82.1 us
    psum x1, waiting for transfers between devices, local(): gate, up = lax.psum((gate_part, up_part), 'row')  63.1 us
    psum x3, blocking collectives, local(): level = lax.psum(squares, 'row') / entries  38.8 us
    dot_general x3, matrix products, local(): lax.dot_general(tangent, down_weight, transposed, preferred_element_type=...  35.5 us
  transfers between devices with their start and end apart: 13, of which 13 were waited for; matrix products, arithmetic and copies ran while one was open for 0% of the time, Pallas kernels for 0%

profile of v1, /device:TPU:0, one launch (start us, length us, event | category | flops | bytes accessed | tf_op | source)
XLA Modules:
  0.0 1036.6 jit_solution(7653385656883551981)
XLA Ops:
  7.2 8.9 fusion.16
  16.2 0.8 copy-done
  17.0 3.6 fusion.17
  20.7 63.1 %all-reduce.15.cloned.1.call-done = (f32[32,7168]{1,0:T(8,128)}, f32[32,7168]{1,0:T(8,128)}) async-done(((f32[32,7168]{1,0:T(8,128)}, f32[32,7168]{1,0:T(8,128)}), (f32[32,7168]{1,0:T(8,128)}, f32[32,7168]{1,0:T(8,128)})) %all-reduce.15.cloned.1.call-update) | async-done | bytes 1835024 | tf_op jit(solution)/shard_map/psum | solution.py:23
  83.7 1.8 fusion.9
  85.6 7.3 bitcast_multiply_fusion.5
  92.8 9.3 fusion
  102.2 47.9 %reduce-scatter.4.cloned.1.call-done = f32[16,7168]{1,0:T(8,128)} async-done(((f32[128,7168]{1,0:T(8,128)}), f32[16,7168]{1,0:T(8,128)}) %reduce-scatter.4.cloned.1.call-update) | async-done | bytes 458768 | tf_op jit(solution)/shard_map/reduce_scatter | solution.py:40
  150.1 1.7 convert_element_type.77
  151.9 27.4 %all-gather.10.cloned.1.call-done = bf16[128,7168]{1,0:T(8,128)(2,1)} async-done(((bf16[16,7168]{1,0:T(8,128)(2,1)}), bf16[128,7168]{1,0:T(8,128)(2,1)}) %all-gather.10.cloned.1.call-update) | async-done | bytes 1835024 | tf_op jit(solution)/shard_map/all_gather | solution.py:44
  179.3 8.6 fusion.18
  187.9 0.3 all-reduce.9.cloned.1.call-start
  188.2 45.5 %all-gather.16.cloned.1.call-done = f32[512,1024]{1,0:T(8,128)} async-done(((f32[128,1024]{1,0:T(8,128)}), f32[512,1024]{1,0:T(8,128)}) %all-gather.16.cloned.1.call-update) | async-done | bytes 2097168 | tf_op jit(solution)/shard_map/all_gather | solution.py:12
  233.7 1.8 reduce_sum.60
  235.5 11.8 %fusion.26 = f32[128,7168]{1,0:T(8,128)} fusion(bf16[128,1024]{1,0:T(8,128)(2,1)S(1)} %reduce_sum.60, bf16[7168,1024]{1,0:T(8,128)(2,1)} %param.10), kind=kOutput, calls=%fused_computation.55 | convolution fusion | flops 1879048192 | bytes 18612224 | tf_op jit(solution)/shard_map/dot_general | solution.py:49
  247.4 78.3 %all-reduce.16 = bf16[128,7168]{1,0:T(8,128)(2,1)} all-reduce(f32[128,7168]{1,0:T(8,128)} %fusion.26), channel_id=1, replica_groups=mesh['row'=8,'col'=4] {'row'}, use_global_device_ids=true, to_apply=%region_4.0 | all-reduce | flops 917504 | bytes 5505024 | tf_op jit(solution)/shard_map/psum | solution.py:52
  325.7 2.1 fusion.6
  327.8 10.1 fusion.19
  338.0 10.9 %convolution_add_fusion.2 = f32[128,1024]{1,0:T(8,128)} fusion(f32[128,1024]{1,0:T(8,128)S(1)} %fusion.19, bf16[128,7168]{1,0:T(8,128)(2,1)S(1)} %get-tuple-element.8, bf16[1024,7168]{1,0:T(8,128)(2,1)} %param.9), kind=kOutput, calls=%fused_computation.23 | convolution fusion | flops 1879179264 | bytes 17563648 | tf_op jit(solution)/shard_map/dot_general | solution.py:58
  348.9 36.5 %all-reduce.9.cloned.1.call-done = f32[128,1024]{1,0:T(8,128)} async-done(((f32[128,1024]{1,0:T(8,128)}), f32[128,1024]{1,0:T(8,128)}) %all-reduce.9.cloned.1.call-update) | async-done | bytes 524304 | tf_op jit(solution)/shard_map/psum | solution.py:61
  385.4 1.2 multiply_reduce_fusion.2
  386.6 0.1 reduce_sum.65
  386.7 0.1 reduce_sum.78
  386.8 13.1 %psum.81 = f32[4]{0:T(128)S(1)} all-reduce(f32[4]{0:T(128)S(1)} %reduce_sum.78), channel_id=1, replica_groups=mesh['row'=8,'col'=4] {'row'}, use_global_device_ids=true, to_apply=%region_8.0 | all-reduce | flops 4 | bytes 32 | tf_op jit(solution)/shard_map/psum | solution.py:64
  400.0 0.1 mul.167
  400.1 7.5 bitcast_multiply_fusion.3
  407.7 9.3 fusion.1
  417.1 46.7 %reduce-scatter.6.cloned.1.call-done = f32[16,7168]{1,0:T(8,128)} async-done(((f32[128,7168]{1,0:T(8,128)}), f32[16,7168]{1,0:T(8,128)}) %reduce-scatter.6.cloned.1.call-update) | async-done | bytes 458768 | tf_op jit(solution)/shard_map/reduce_scatter | solution.py:40
  463.7 1.7 convert_element_type.84
  465.5 27.4 %all-gather.12.cloned.1.call-done = bf16[128,7168]{1,0:T(8,128)(2,1)} async-done(((bf16[16,7168]{1,0:T(8,128)(2,1)}), bf16[128,7168]{1,0:T(8,128)(2,1)}) %all-gather.12.cloned.1.call-update) | async-done | bytes 1835024 | tf_op jit(solution)/shard_map/all_gather | solution.py:44
  492.9 8.6 fusion.20
  501.6 45.8 %all-gather.18.cloned.1.call-done = f32[512,1024]{1,0:T(8,128)} async-done(((f32[128,1024]{1,0:T(8,128)}), f32[512,1024]{1,0:T(8,128)}) %all-gather.18.cloned.1.call-update) | async-done | bytes 2097168 | tf_op jit(solution)/shard_map/all_gather | solution.py:12
  547.3 1.8 reduce_sum.79
  549.1 11.8 %fusion.25 = f32[128,7168]{1,0:T(8,128)} fusion(bf16[128,1024]{1,0:T(8,128)(2,1)S(1)} %reduce_sum.79, bf16[7168,1024]{1,0:T(8,128)(2,1)} %param.10), kind=kOutput, calls=%fused_computation.54 | convolution fusion | flops 1879048192 | bytes 18612224 | tf_op jit(solution)/shard_map/dot_general | solution.py:49
  561.0 78.5 %all-reduce.17 = bf16[128,7168]{1,0:T(8,128)(2,1)} all-reduce(f32[128,7168]{1,0:T(8,128)} %fusion.25), channel_id=1, replica_groups=mesh['row'=8,'col'=4] {'row'}, use_global_device_ids=true, to_apply=%region_11.0 | all-reduce | flops 917504 | bytes 5505024 | tf_op jit(solution)/shard_map/psum | solution.py:52
  639.5 2.1 fusion.7
  641.6 10.1 fusion.21
  651.7 10.9 %convolution_add_fusion.1 = f32[128,1024]{1,0:T(8,128)} fusion(f32[128,1024]{1,0:T(8,128)S(1)} %fusion.21, bf16[128,7168]{1,0:T(8,128)(2,1)S(1)} %get-tuple-element.6, bf16[1024,7168]{1,0:T(8,128)(2,1)} %param.9), kind=kOutput, calls=%fused_computation.22 | convolution fusion | flops 1879179264 | bytes 17563648 | tf_op jit(solution)/shard_map/dot_general | solution.py:58
  662.7 36.5 %all-reduce.11.cloned.1.call-done = f32[128,1024]{1,0:T(8,128)} async-done(((f32[128,1024]{1,0:T(8,128)}), f32[128,1024]{1,0:T(8,128)}) %all-reduce.11.cloned.1.call-update) | async-done | bytes 524304 | tf_op jit(solution)/shard_map/psum | solution.py:61
  699.2 1.2 multiply_reduce_fusion.1
  700.4 0.1 reduce_sum.81
  700.5 0.1 reduce_sum.82
  700.6 12.9 %psum.84 = f32[4]{0:T(128)S(1)} all-reduce(f32[4]{0:T(128)S(1)} %reduce_sum.82), channel_id=1, replica_groups=mesh['row'=8,'col'=4] {'row'}, use_global_device_ids=true, to_apply=%region_15.0 | all-reduce | flops 4 | bytes 32 | tf_op jit(solution)/shard_map/psum | solution.py:64
  713.6 0.1 mul.178
  713.7 7.5 bitcast_multiply_fusion.1
  721.3 9.3 fusion.2
  730.7 46.7 %reduce-scatter.8.cloned.1.call-done = f32[16,7168]{1,0:T(8,128)} async-done(((f32[128,7168]{1,0:T(8,128)}), f32[16,7168]{1,0:T(8,128)}) %reduce-scatter.8.cloned.1.call-update) | async-done | bytes 458768 | tf_op jit(solution)/shard_map/reduce_scatter | solution.py:40
  777.3 1.7 convert_element_type.91
  779.1 27.4 %all-gather.14.cloned.1.call-done = bf16[128,7168]{1,0:T(8,128)(2,1)} async-done(((bf16[16,7168]{1,0:T(8,128)(2,1)}), bf16[128,7168]{1,0:T(8,128)(2,1)}) %all-gather.14.cloned.1.call-update) | async-done | bytes 1835024 | tf_op jit(solution)/shard_map/all_gather | solution.py:44
  806.5 8.6 fusion.22
  815.2 45.8 %all-gather.20.cloned.1.call-done = f32[512,1024]{1,0:T(8,128)} async-done(((f32[128,1024]{1,0:T(8,128)}), f32[512,1024]{1,0:T(8,128)}) %all-gather.20.cloned.1.call-update) | async-done | bytes 2097168 | tf_op jit(solution)/shard_map/all_gather | solution.py:12
  860.9 1.8 reduce_sum.83
  862.8 11.8 %fusion.24 = f32[128,7168]{1,0:T(8,128)} fusion(bf16[128,1024]{1,0:T(8,128)(2,1)S(1)} %reduce_sum.83, bf16[7168,1024]{1,0:T(8,128)(2,1)} %param.10), kind=kOutput, calls=%fused_computation.53 | convolution fusion | flops 1879048192 | bytes 18612224 | tf_op jit(solution)/shard_map/dot_general | solution.py:49
  874.6 78.6 %all-reduce.18 = bf16[128,7168]{1,0:T(8,128)(2,1)} all-reduce(f32[128,7168]{1,0:T(8,128)} %fusion.24), channel_id=1, replica_groups=mesh['row'=8,'col'=4] {'row'}, use_global_device_ids=true, to_apply=%region_18.0 | all-reduce | flops 917504 | bytes 5505024 | tf_op jit(solution)/shard_map/psum | solution.py:52
  953.2 2.1 fusion.8
  955.3 10.1 fusion.23
  965.4 10.9 %convolution_add_fusion = f32[128,1024]{1,0:T(8,128)} fusion(f32[128,1024]{1,0:T(8,128)S(1)} %fusion.23, bf16[128,7168]{1,0:T(8,128)(2,1)S(1)} %get-tuple-element.4, bf16[1024,7168]{1,0:T(8,128)(2,1)} %param.9), kind=kOutput, calls=%fused_computation.21 | convolution fusion | flops 1879179264 | bytes 17563648 | tf_op jit(solution)/shard_map/dot_general | solution.py:58
  976.4 36.7 %all-reduce.13.cloned.1.call-done = f32[128,1024]{1,0:T(8,128)} async-done(((f32[128,1024]{1,0:T(8,128)}), f32[128,1024]{1,0:T(8,128)}) %all-reduce.13.cloned.1.call-update) | async-done | bytes 524304 | tf_op jit(solution)/shard_map/psum | solution.py:61
  1013.0 1.2 multiply_reduce_fusion
  1014.2 0.1 reduce_sum.85
  1014.3 0.1 reduce_sum.86
  1014.4 12.7 %psum.87 = f32[4]{0:T(128)S(1)} all-reduce(f32[4]{0:T(128)S(1)} %reduce_sum.86), channel_id=1, replica_groups=mesh['row'=8,'col'=4] {'row'}, use_global_device_ids=true, to_apply=%region_22.23 | all-reduce | flops 4 | bytes 32 | tf_op jit(solution)/shard_map/psum | solution.py:64
  1027.1 0.5 multiply_sqrt_fusion
  1027.6 2.0 multiply_multiply_fusion.1
  (41 shorter events, 0.9 us)
Async XLA Ops:
  7.2 9.0 copy-start.3
  7.2 9.0 copy-start.5
  7.2 76.6 %all-reduce.15.cloned.1.call-start = ((), (), s32[]{:S(2)}) async-start(), calls=%async_computation.15 | async-start | bytes 3670016 | tf_op jit(solution)/shard_map/psum | solution.py:23
  7.2 9.7 copy-start
  17.0 3.7 copy-start.4
  20.6 129.5 %reduce-scatter.4.cloned.1.call-start = ((), (), s32[]{:S(2)}) async-start(), calls=%async_computation.3 | async-start | bytes 4128768 | tf_op jit(solution)/shard_map/reduce_scatter | solution.py:40
  102.2 77.1 %all-gather.10.cloned.1.call-start = ((), (), s32[]{:S(2)}) async-start(), calls=%async_computation.4 | async-start | bytes 2064384 | tf_op jit(solution)/shard_map/all_gather | solution.py:44
  151.8 81.9 %all-gather.16.cloned.1.call-start = ((), (), s32[]{:S(2)}) async-start(), calls=%async_computation.12 | async-start | bytes 2621440 | tf_op jit(solution)/shard_map/all_gather | solution.py:12
  187.9 197.5 %all-reduce.9.cloned.1.call-start = ((), (), s32[]{:S(2)}) async-start(), calls=%async_computation.5 | async-start | bytes 1048576 | tf_op jit(solution)/shard_map/psum | solution.py:61
  348.9 114.9 %reduce-scatter.6.cloned.1.call-start = ((), (), s32[]{:S(2)}) async-start(), calls=%async_computation.6 | async-start | bytes 4128768 | tf_op jit(solution)/shard_map/reduce_scatter | solution.py:40
  400.1 7.6 copy-start.1
  417.0 75.9 %all-gather.12.cloned.1.call-start = ((), (), s32[]{:S(2)}) async-start(), calls=%async_computation.7 | async-start | bytes 2064384 | tf_op jit(solution)/shard_map/all_gather | solution.py:44
  465.5 81.8 %all-gather.18.cloned.1.call-start = ((), (), s32[]{:S(2)}) async-start(), calls=%async_computation.13 | async-start | bytes 2621440 | tf_op jit(solution)/shard_map/all_gather | solution.py:12
  501.5 197.7 %all-reduce.11.cloned.1.call-start = ((), (), s32[]{:S(2)}) async-start(), calls=%async_computation.8 | async-start | bytes 1048576 | tf_op jit(solution)/shard_map/psum | solution.py:61
  662.7 114.7 %reduce-scatter.8.cloned.1.call-start = ((), (), s32[]{:S(2)}) async-start(), calls=%async_computation.9 | async-start | bytes 4128768 | tf_op jit(solution)/shard_map/reduce_scatter | solution.py:40
  713.7 7.6 copy-start.2
  730.6 75.9 %all-gather.14.cloned.1.call-start = ((), (), s32[]{:S(2)}) async-start(), calls=%async_computation.10 | async-start | bytes 2064384 | tf_op jit(solution)/shard_map/all_gather | solution.py:44
  779.1 81.9 %all-gather.20.cloned.1.call-start = ((), (), s32[]{:S(2)}) async-start(), calls=%async_computation.14 | async-start | bytes 2621440 | tf_op jit(solution)/shard_map/all_gather | solution.py:12
  815.1 197.9 %all-reduce.13.cloned.1.call-start = ((), (), s32[]{:S(2)}) async-start(), calls=%async_computation.11 | async-start | bytes 1048576 | tf_op jit(solution)/shard_map/psum | solution.py:61
Sparse Core Ops, SparseCore 0:
  20.7 63.0 all-reduce.14
  102.3 47.7 reduce-scatter.3
  152.6 26.6 all-gather.9
  188.0 45.6 all-gather.15
  349.0 36.3 all-reduce.8
  417.1 46.5 reduce-scatter.5
  466.2 26.6 all-gather.11
  501.6 45.6 all-gather.17
  662.8 36.3 all-reduce.10
  730.7 46.5 reduce-scatter.7
  779.8 26.6 all-gather.13
  815.2 45.6 all-gather.19
  976.5 36.4 all-reduce.12
